TPU v7x, 32 devices: a whole 2x2x4 slice. The times are simulated.
32 devices in a mesh: seq: 8 (over y, x, core), tensor: 4 (over z).
Axes of the slice: x: 2, y: 2, z: 4, core: 2. Of those that a mesh axis runs over, the one named last changes fastest.
Arguments:
- tokens: bfloat16 [5760, 1536], P('seq'), may hold values from -6 to 6
- norm_gain: float32 [1536], replicated, may hold values from 0.1 to 1.9
- w_qkv: bfloat16 [1536, 3, 1536], P(None, None, 'tensor'), may hold values from -8 to 8
- w_out: bfloat16 [1536, 1536], P('tensor'), may hold values from -0.15625 to 0.15625
- post_gain: float32 [1536], replicated, may hold values from 0.1 to 1.9
- w_up: bfloat16 [1536, 6144], P(None, 'tensor'), may hold values from -0.15625 to 0.15625
- w_down: bfloat16 [6144, 1536], P('tensor'), may hold values from -0.078125 to 0.078125
Outputs:
- layer_out: bfloat16 [5760, 1536], P('seq')
All inputs are finite; a program needn't handle non-finite values.
Results may differ from a plain program's by a relative error of at most 0.015.
Values may be sent and summed in bfloat16 or wider, within the bound.
A program may use at most 128 MiB of HBM per device.

v0:
```python
import functools

import jax
import jax.numpy as jnp
from jax import lax
from jax.experimental import pallas as pl
from jax.experimental.pallas import tpu as pltpu
from jax.sharding import PartitionSpec as P

HD = 48
ONES = 16
LOG2E = 1.4426950408889634
MESH = pl.DeviceIdType.MESH
CONTRACT_FIRST = (((0,), (0,)), ((), ()))


def layer_norm(values, gain):
    mean = jnp.mean(values, axis=-1, keepdims=True)
    centred = values - mean
    var = jnp.mean(centred * centred, axis=-1, keepdims=True)
    return centred * lax.rsqrt(var + 1e-05) * gain


def flip(chip, mask, chips):
    result, bit = 0, 1
    while bit < chips:
        mine, other = (chip // bit) % 2, (mask // bit) % 2
        result = result + bit * (mine + other - 2 * mine * other)
        bit *= 2
    return result


def layer_kernel(
    n, lanes, parts, chunk, sub,
    q_ref, kv_ref, tokens_ref, gain_ref, shard_ref, up_ref, down_ref, o_ref,
    held, score_a, score_b, column, accum, peak, att, wo, wu, wd, mixed, term, inbox, res,
    load_sem, recv_sem, send_sem, pass_sem, wide_send, wide_recv, part_send, part_pass, part_recv,
    block_sem, right_sem, left_sem, in_send, in_sem, out_send, out_sem, store_sem,
):
    seq, lane = lax.axis_index("seq"), lax.axis_index("tensor")
    chips = n // 2
    bits = chips.bit_length() - 1
    chip, core = seq // 2, seq % 2
    sibling = chip * 2 + 1 - core
    rows = tokens_ref.shape[0]
    groups = kv_ref.shape[0]
    size = kv_ref.shape[1] // 2
    width = size * HD

    def when(*conditions):
        return pl.when(functools.reduce(jnp.logical_and, conditions))

    def remote(source, target, send, recv, device):
        return pltpu.make_async_remote_copy(
            src_ref=source, dst_ref=target, send_sem=send, recv_sem=recv, device_id=device, device_id_type=MESH
        )

    def slot_of(arrival, which):
        turned = sum((arrival // 2**i) % 2 * 2 ** (bits - 1 - i) for i in range(bits))
        return flip(chip, jnp.where(which == 0, arrival, turned), chips) * 2 + which

    def partner(stage):
        return flip(chip, jnp.where(core == 0, 2**stage, 2 ** (bits - 1 - stage)), chips) * 2 + core

    def exchange(group, arrival, stage):
        slot = slot_of(arrival, core)
        block = held.at[slot, group]
        return remote(
            block, block, send_sem.at[stage, group, arrival], recv_sem.at[slot, group], (partner(stage), lane)
        )

    def hand(group, arrival, which):
        slot = slot_of(arrival, which)
        block = held.at[slot, group]
        return remote(block, block, pass_sem.at[group, arrival], recv_sem.at[slot, group], (sibling, lane))

    part = seq % parts
    extent = shard_ref.shape[0] // parts
    mates = parts // 2
    first = chip // mates * mates

    def rows_of(index):
        return pl.ds(pl.multiple_of(index * extent, extent), extent)

    def wide(source, step):
        strip = wo.at[source, rows_of(part)]
        return remote(strip, strip, wide_send.at[step], wide_recv.at[source], (seq, (lane + step) % lanes))

    def mate(step):
        return first + (chip - first + step) % mates

    def spread(source, step):
        strip = wo.at[source, rows_of(part)]
        return remote(
            strip, strip, part_send.at[source, step], part_recv.at[source, part], (mate(step) * 2 + core, lane)
        )

    def share(source, index):
        strip = wo.at[source, rows_of(index)]
        return remote(strip, strip, part_pass.at[source, index], part_recv.at[source, index], (sibling, lane))

    def block(source, group, target, sem):
        rows_here = pl.ds(pl.multiple_of(group * width, width), width)
        piece_ref = att.at[source, rows_here]
        return remote(piece_ref, piece_ref, sem.at[source, group], block_sem.at[source, group], (seq, target))

    has_left, has_right = lane > 0, lane < lanes - 1

    def relay_blocks(group, distance):
        live = jnp.logical_and(group >= 0, group < groups)
        if distance == 0:
            @when(live, has_right)
            def _():
                block(lane, group, lane + 1, right_sem).start()

            @when(live, has_left)
            def _():
                block(lane, group, lane - 1, left_sem).start()

            return

        @when(live, lane - distance >= 0)
        def _():
            block(lane - distance, group, lane + 1, right_sem).wait_recv()

        @when(live, lane - distance >= 0, has_right)
        def _():
            block(lane - distance, group, lane + 1, right_sem).start()

        @when(live, lane + distance < lanes)
        def _():
            block(lane + distance, group, lane - 1, left_sem).wait_recv()

        @when(live, lane + distance < lanes, has_left)
        def _():
            block(lane + distance, group, lane - 1, left_sem).start()

    def tick_middle(group):
        for distance in range(1, lanes, 2):
            relay_blocks(group - (distance + 1) // 2, distance)

    def tick_end(group):
        for distance in range(0, lanes, 2):
            relay_blocks(group - distance // 2, distance)

    barrier = pltpu.get_barrier_semaphore()
    pl.semaphore_signal(barrier, inc=1, device_id=(sibling, lane), device_id_type=MESH)
    for step in range(1, chips):
        pl.semaphore_signal(
            barrier, inc=1, device_id=(flip(chip, step, chips) * 2 + core, lane), device_id_type=MESH
        )
    for step in range(1, lanes):
        pl.semaphore_signal(barrier, inc=1, device_id=(seq, (lane + step) % lanes), device_id_type=MESH)

    own = pltpu.make_async_copy(kv_ref, held.at[seq], load_sem.at[0])
    own.start()
    own_shard = pltpu.make_async_copy(shard_ref, wo.at[lane], load_sem.at[1])
    own_shard.start()
    loads = [
        pltpu.make_async_copy(up_ref, wu, load_sem.at[2]),
        pltpu.make_async_copy(down_ref, wd, load_sem.at[3]),
    ]
    for load in loads:
        load.start()
    own.wait()
    pl.semaphore_wait(barrier, chips + lanes - 1)

    def open_group(group):
        exchange(group, 0, 0).start()
        hand(group, 0, core).start()

    open_group(0)
    own_shard.wait()
    for step in range(1, lanes):
        wide(lane, step).start()

    def prepare(group, index):
        arrival, second = index // 2, index % 2
        which = core + second - 2 * core * second
        hand(group, arrival, which).wait_recv()

        @pl.when(second == 0)
        def _():
            hand(group, arrival, core).start()
            for stage in range(1, bits):
                @pl.when(arrival < 2**stage)
                def _():
                    exchange(group, arrival, stage).start()

        @when(second == 0, arrival == 1)
        def _():
            for stage in range(1, bits):
                exchange(group, 0, stage).start()

            @pl.when(group + 1 < groups)
            def _():
                open_group(group + 1)

    def score(slot, group, member, target):
        result = lax.dot_general(
            held[slot, group, member], q_ref[group * size + member], CONTRACT_FIRST,
            preferred_element_type=jnp.float32,
        )
        target[...] = result
        return jnp.max(result, axis=0, keepdims=True)

    def attend(slot, group, member, source, top):
        value = held[slot, group, size + member]
        value = jnp.concatenate([value, jnp.ones((ONES, rows), value.dtype)], axis=0)
        old = peak[member]
        new = jnp.maximum(old, top)
        weights = jnp.exp2(source[...] - new).astype(jnp.bfloat16)
        term_here = jnp.dot(value, weights, preferred_element_type=jnp.float32)
        accum[member] = accum[member] * jnp.exp2(old - new) + term_here
        peak[member] = new

    scores = (score_a, score_b)
    column[...] = score(seq, 0, 0, score_a)

    @pl.loop(0, groups)
    def _(group):
        accum[...] = jnp.zeros_like(accum)
        peak[...] = jnp.full_like(peak, -1e30)

        @pl.loop(0, n)
        def _(index):
            def place(position):
                arrival, second = position // 2, position % 2
                return slot_of(arrival, core + second - 2 * core * second)

            @pl.when(index == chips)
            def _():
                tick_middle(group)

            @when(index == 3, group == groups - 1)
            def _():
                for step in range(1, lanes):
                    source = (lane + step) % lanes
                    wide(source, step).wait_recv()
                    share(source, part).start()
                    for other in range(1, mates):
                        spread(source, other).start()

            slot = place(index)
            for member in range(size):
                top = column[...]
                if member < size - 1:
                    below = score(slot, group, member + 1, scores[(member + 1) % 2])
                else:
                    @pl.when(index + 1 < n)
                    def _():
                        prepare(group, index + 1)

                    last = index + 1 == n
                    following = jnp.where(last, seq, place((index + 1) % n))
                    next_group = jnp.minimum(group + jnp.where(last, 1, 0), groups - 1)
                    below = score(following, next_group, 0, scores[(member + 1) % 2])
                attend(slot, group, member, scores[member % 2], top)
                column[...] = below

        for member in range(size):
            rows_here = pl.ds(pl.multiple_of(group * width + member * HD, HD), HD)
            att[lane, rows_here, :] = (accum[member, :HD] / accum[member, HD : HD + 1]).astype(att.dtype)
        tick_end(group)

    for group in range(groups, groups + lanes // 2 + 1):
        tick_middle(group)
        tick_end(group)

    for step in range(1, lanes):
        source = (lane + step) % lanes
        for other in range(1, mates):
            index = (mate(other) * 2 + core) % parts
            share(source, index).wait_recv()
            share(source, index).start()
    for step in range(1, lanes):
        source = (lane + step) % lanes
        for other in range(mates):
            share(source, (mate(other) * 2 + 1 - core) % parts).wait_recv()
    for load in loads:
        load.wait()

    full, rest = rows // chunk, rows % chunk
    chunks, per, pieces = full + (rest > 0), chunk // sub, rows // sub
    middle = lanes // 2
    on_left = lane < middle
    depth = jnp.where(on_left, lane, lanes - 1 - lane)
    inner = jnp.where(on_left, lane + 1, lane - 1)
    outer = jnp.where(on_left, lane - 1, lane + 1)
    central = depth == middle - 1

    def piece(index):
        return pl.ds(pl.multiple_of(index * sub, sub), sub)

    def inward(index, box):
        return remote(
            term.at[piece(index)], inbox.at[box, piece(index)],
            in_send.at[index], in_sem.at[box, index], (seq, inner),
        )

    def outward(index):
        return remote(
            res.at[piece(index)], res.at[piece(index)], out_send.at[index], out_sem.at[index], (seq, outer)
        )

    def store(index):
        return pltpu.make_async_copy(res.at[piece(index)], o_ref.at[piece(index)], store_sem.at[index])

    def compute(start, count):
        span = pl.ds(start, count)
        attended = att[:, :, span].reshape(-1, count)
        total = tokens_ref[span, :].astype(jnp.float32) + lax.dot_general(
            attended, wo[...].reshape(-1, wo.shape[2]), CONTRACT_FIRST, preferred_element_type=jnp.float32
        )
        mixed[span, :] = total
        post = layer_norm(total, gain_ref[...]).astype(jnp.bfloat16)
        hidden = jax.nn.gelu(
            jnp.dot(post, wu[...], preferred_element_type=jnp.float32), approximate=True
        ).astype(jnp.bfloat16)
        term[span, :] = jnp.dot(hidden, wd[...], preferred_element_type=jnp.float32).astype(jnp.bfloat16)

    def reduce_inward(index):
        @pl.when(depth > 0)
        def _():
            inward(index, 0).wait_recv()
            rows_here = piece(index)
            term[rows_here, :] = (
                term[rows_here, :].astype(jnp.float32) + inbox[0, rows_here, :].astype(jnp.float32)
            ).astype(jnp.bfloat16)

        inward(index, jnp.where(central, 1, 0)).start()

    def finish(index):
        inward(index, 1).wait_recv()
        rows_here = piece(index)
        both = term[rows_here, :].astype(jnp.float32) + inbox[1, rows_here, :].astype(jnp.float32)
        res[rows_here, :] = (mixed[rows_here, :] + both).astype(jnp.bfloat16)

        @pl.when(depth > 0)
        def _():
            outward(index).start()

        store(index).start()

    def relay(index):
        outward(index).wait_recv()

        @pl.when(depth > 0)
        def _():
            outward(index).start()

        store(index).start()

    def each(step, body):
        @pl.when(jnp.logical_and(step >= 0, step < chunks))
        def _():
            @pl.loop(step * per, jnp.minimum(step * per + per, pieces))
            def _(index):
                body(index)

    @pl.loop(0, chunks + lanes - 1)
    def _(step):
        @pl.when(step < full)
        def _():
            compute(pl.multiple_of(step * chunk, chunk), chunk)

        if rest:
            @pl.when(step == full)
            def _():
                compute(full * chunk, rest)

        each(step - depth, reduce_inward)

        @pl.when(central)
        def _():
            each(step - middle, finish)

        @when(jnp.logical_not(central), depth > 0)
        def _():
            each(step - middle - (middle - 1 - depth), relay)

    @when(jnp.logical_not(central), depth == 0)
    def _():
        @pl.loop(0, pieces)
        def _(index):
            relay(index)

    @pl.loop(0, groups)
    def _(group):
        for source in range(lanes):
            @when(lane >= source, has_right)
            def _():
                block(source, group, lane + 1, right_sem).wait_send()

            @when(lane <= source, has_left)
            def _():
                block(source, group, lane - 1, left_sem).wait_send()

        for arrival in range(chips):
            hand(group, arrival, core).wait_send()
            for stage in range(bits):
                if arrival < 2**stage:
                    exchange(group, arrival, stage).wait_send()

    for step in range(1, lanes):
        wide(lane, step).wait_send()
        source = (lane + step) % lanes
        share(source, part).wait_send()
        for other in range(1, mates):
            spread(source, other).wait_send()
            share(source, (mate(other) * 2 + core) % parts).wait_send()

    @pl.loop(0, pieces)
    def _(index):
        inward(index, 0).wait_send()
        store(index).wait()

        @pl.when(depth > 0)
        def _():
            outward(index).wait_send()


def fused(n, lanes, query, pairs, tokens, gain, w_out, w_up, w_down):
    rows, width = tokens.shape
    span, hidden = w_out.shape[0], w_up.shape[1]
    heads = span // HD
    groups, size = pairs.shape[0], pairs.shape[1] // 2
    parts = n
    while span // parts % 16 or span % parts:
        parts //= 2
    chips = n // 2
    bits = chips.bit_length() - 1
    chunk, sub = 128, 16
    pieces = rows // sub
    vmem = pl.BlockSpec(memory_space=pltpu.VMEM)
    hbm = pl.BlockSpec(memory_space=pl.ANY)
    dma = pltpu.SemaphoreType.DMA
    return pl.pallas_call(
        functools.partial(layer_kernel, n, lanes, parts, chunk, sub),
        out_shape=jax.ShapeDtypeStruct((rows, width), jnp.bfloat16),
        in_specs=[vmem, vmem, vmem, vmem, hbm, hbm, hbm],
        out_specs=hbm,
        scratch_shapes=[
            pltpu.VMEM((n, groups, 2 * size, HD, rows), jnp.bfloat16),
            pltpu.VMEM((rows, rows), jnp.float32),
            pltpu.VMEM((rows, rows), jnp.float32),
            pltpu.VMEM((1, rows), jnp.float32),
            pltpu.VMEM((size, HD + ONES, rows), jnp.float32),
            pltpu.VMEM((size, 1, rows), jnp.float32),
            pltpu.VMEM((lanes, span, rows), jnp.bfloat16),
            pltpu.VMEM((lanes, span, width), jnp.bfloat16),
            pltpu.VMEM((width, hidden), jnp.bfloat16),
            pltpu.VMEM((hidden, width), jnp.bfloat16),
            pltpu.VMEM((rows, width), jnp.float32),
            pltpu.VMEM((rows, width), jnp.bfloat16),
            pltpu.VMEM((2, rows, width), jnp.bfloat16),
            pltpu.VMEM((rows, width), jnp.bfloat16),
            dma((4,)),
            dma((n, groups)),
            dma((bits, groups, chips)),
            dma((groups, chips)),
            dma((lanes,)),
            dma((lanes,)),
            dma((lanes, parts // 2)),
            dma((lanes, parts)),
            dma((lanes, parts)),
            dma((lanes, groups)),
            dma((lanes, groups)),
            dma((lanes, groups)),
            dma((pieces,)),
            dma((2, pieces)),
            dma((pieces,)),
            dma((pieces,)),
            dma((pieces,)),
        ],
        compiler_params=pltpu.CompilerParams(
            collective_id=0, has_side_effects=True, vmem_limit_bytes=63 * 2**20
        ),
        cost_estimate=pl.CostEstimate(
            flops=4 * n * heads * rows * rows * HD + 2 * rows * width * (lanes * span + 2 * hidden),
            bytes_accessed=2 * width * (lanes * span + 2 * hidden),
            transcendentals=n * heads * rows * rows,
        ),
    )(query, pairs, tokens, gain, w_out, w_up, w_down)


def per_device(n, lanes, tokens, norm_gain, w_qkv, w_out, post_gain, w_up, w_down):
    rows = tokens.shape[0]
    span = w_qkv.shape[2]
    heads = span // HD
    base = tokens.astype(jnp.float32)
    normed = layer_norm(base, norm_gain).astype(jnp.bfloat16)
    weights = w_qkv.reshape(w_qkv.shape[0], -1)
    qkv = lax.dot_general(weights, normed, (((0,), (1,)), ((), ())), preferred_element_type=jnp.float32)
    query = (qkv[:span] * (LOG2E / HD**0.5)).astype(jnp.bfloat16).reshape(heads, HD, rows)
    pairs = qkv[span:].astype(jnp.bfloat16).reshape(2, heads // 2, 2, HD, rows)
    pairs = pairs.transpose(1, 0, 2, 3, 4).reshape(heads // 2, 4, HD, rows)
    return fused(n, lanes, query, pairs, tokens, post_gain.reshape(1, -1), w_out, w_up, w_down)


def solution(mesh):
    placed = (
        P("seq", None),
        P(),
        P(None, None, "tensor"),
        P("tensor", None),
        P(),
        P(None, "tensor"),
        P("tensor", None),
    )
    return jax.shard_map(
        functools.partial(per_device, mesh.shape["seq"], mesh.shape["tensor"]),
        mesh=mesh,
        in_specs=placed,
        out_specs=P("seq", None),
        check_vma=False,
    )
```

profile of v0, /device:TPU:0, one launch (start us, length us, event | category | flops | bytes accessed | tf_op | source)
XLA Modules:
  0.0 216.8 jit_solution(4121352929567552788)
XLA Ops:
  0.0 0.0 copy-start
  0.0 2.1 convert_reduce_fusion
  2.1 0.1 copy-done
  2.3 0.7 fusion.2
  3.0 0.0 copy-start.2
  3.0 6.1 %copy.10 = bf16[1536,3,384]{0,2,1:T(8,128)(2,1)} copy(bf16[1536,3,384]{2,0,1:T(8,128)(2,1)} %param.9) | data formatting | bytes 7077888 | tf_op args[2]
  9.1 0.0 copy-done.2
  9.1 6.9 %convolution_bitcast_fusion = f32[1152,720]{0,1:T(8,128)} fusion(bf16[1536,1152]{0,1:T(8,128)(2,1)} %bitcast.10, bf16[720,1536]{1,0:T(8,128)(2,1)S(1)} %copy-done, f32[1536]{0:T(1024)S(1)} %copy-done.2, f32[720]{0:T(1024)S(1)} %add_rsqrt_fusion, f32[720]{0:T(1024)S(1)} %broadcast_multiply_fusion), kind=kOutput, calls=%fused_computation.7 | convolution fusion | flops 2553569280 | bytes 9080448 | tf_op jit(solution)/shard_map/dot_general | solution.py:494
  16.0 1.7 slice.15
  17.7 0.0 copy-start.1
  17.7 0.6 copy.12
  18.4 1.1 copy.13
  19.5 1.3 fusion.9
  20.8 1.1 copy.11
  21.9 0.0 copy-done.1
  21.9 0.6 reshape.32.gain_ref
  22.5 191.1 %shard_map.73 = bf16[720,1536]{1,0:T(8,128)(2,1)} custom-call(bf16[8,48,720]{2,1,0:T(8,128)(2,1)} %bitcast.12, bf16[4,4,48,720]{3,2,1,0:T(8,128)(2,1)} %bitcast.11, bf16[720,1536]{1,0:T(8,128)(2,1)} %tokens_ref.1, f32[1,1536]{1,0:T(1,128)} %reshape.32.gain_ref, bf16[384,1536]{1,0:T(8,128)(2,1)} %shard_ref.1, bf16[1536,1536]{1,0:T(8,128)(2,1)} %up_ref.1, ...), custom_call_target="tpu_custom_call" | custom-call | flops 16562257920 | bytes 14155776 | tf_op jit(solution)/shard_map/pallas_call | solution.py:438
  213.7 3.1 %copy.15 = bf16[720,1536]{1,0:T(8,128)(2,1)} copy(bf16[720,1536]{1,0:T(8,128)(2,1)} %shard_map.73) | data formatting | bytes 4423680
  (2 shorter events, 0.0 us)
Async XLA Ops:
  0.0 2.3 %copy-start = (bf16[720,1536]{1,0:T(8,128)(2,1)S(1)}, bf16[720,1536]{1,0:T(8,128)(2,1)}, u32[]{:S(2)}) copy-start(bf16[720,1536]{1,0:T(8,128)(2,1)} %tokens_ref.1) | copy-start | bytes 6635524
  3.0 6.1 %copy-start.2 = (f32[1536]{0:T(1024)S(1)}, f32[1536]{0:T(1024)}, u32[]{:S(2)}) copy-start(f32[1536]{0:T(1024)} %param.8) | copy-start | bytes 18436
  17.7 4.2 %copy-start.1 = (f32[1536]{0:T(1024)S(1)}, f32[1536]{0:T(1024)}, u32[]{:S(2)}) copy-start(f32[1536]{0:T(1024)} %param.11) | copy-start | bytes 18436
where the time goes:
time: 218 us; the launch traced here: 217 us
  Pallas kernels  191 us (88%)
  local copies, waits for them, and re-layouts  14.5 us (7%)
  matrix products  6.89 us (3%)
  other arithmetic  4.2 us (2%)
    pallas_call x1, Pallas kernels, fused(): pl.pallas_call(functools.partial(layer_kernel, n, lanes, parts, chunk, su...  191 us
    unnamed x8, local copies, waits for them, and re-layouts  9.36 us
    dot_general x1, matrix products, per_device(): lax.dot_general(weights, normed, (((0,), (1,)), ((), ())), preferred_elem...  6.89 us

commit v1 on v0

--- a/solution.py
+++ b/solution.py
@@ -32,10 +32,10 @@
 
 def layer_kernel(
     n, lanes, parts, chunk, sub,
-    q_ref, kv_ref, tokens_ref, gain_ref, shard_ref, up_ref, down_ref, o_ref,
-    held, score_a, score_b, column, accum, peak, att, wo, wu, wd, mixed, term, inbox, res,
+    groups, size, tokens_ref, first_gain_ref, qkv_ref, gain_ref, shard_ref, up_ref, down_ref, o_ref,
+    query, wq, held, score_a, score_b, column, accum, peak, att, wo, wu, wd, mixed, term, inbox, res,
     load_sem, recv_sem, send_sem, pass_sem, wide_send, wide_recv, part_send, part_pass, part_recv,
-    block_sem, right_sem, left_sem, in_send, in_sem, out_send, out_sem, store_sem,
+    block_sem, block_send, relay_send, in_send, in_sem, out_send, out_sem, store_sem,
 ):
     seq, lane = lax.axis_index("seq"), lax.axis_index("tensor")
     chips = n // 2
@@ -43,8 +43,6 @@
     chip, core = seq // 2, seq % 2
     sibling = chip * 2 + 1 - core
     rows = tokens_ref.shape[0]
-    groups = kv_ref.shape[0]
-    size = kv_ref.shape[1] // 2
     width = size * HD
 
     def when(*conditions):
@@ -99,49 +97,33 @@
         strip = wo.at[source, rows_of(index)]
         return remote(strip, strip, part_pass.at[source, index], part_recv.at[source, index], (sibling, lane))
 
-    def block(source, group, target, sem):
+    def block(source, group, distance):
         rows_here = pl.ds(pl.multiple_of(group * width, width), width)
-        piece_ref = att.at[source, rows_here]
-        return remote(piece_ref, piece_ref, sem.at[source, group], block_sem.at[source, group], (seq, target))
-
-    has_left, has_right = lane > 0, lane < lanes - 1
-
-    def relay_blocks(group, distance):
-        live = jnp.logical_and(group >= 0, group < groups)
-        if distance == 0:
-            @when(live, has_right)
-            def _():
-                block(lane, group, lane + 1, right_sem).start()
-
-            @when(live, has_left)
-            def _():
-                block(lane, group, lane - 1, left_sem).start()
-
-            return
-
-        @when(live, lane - distance >= 0)
-        def _():
-            block(lane - distance, group, lane + 1, right_sem).wait_recv()
-
-        @when(live, lane - distance >= 0, has_right)
-        def _():
-            block(lane - distance, group, lane + 1, right_sem).start()
-
-        @when(live, lane + distance < lanes)
-        def _():
-            block(lane + distance, group, lane - 1, left_sem).wait_recv()
-
-        @when(live, lane + distance < lanes, has_left)
-        def _():
-            block(lane + distance, group, lane - 1, left_sem).start()
-
-    def tick_middle(group):
-        for distance in range(1, lanes, 2):
-            relay_blocks(group - (distance + 1) // 2, distance)
-
-    def tick_end(group):
-        for distance in range(0, lanes, 2):
-            relay_blocks(group - distance // 2, distance)
+        strip = att.at[source, rows_here]
+        return remote(
+            strip, strip, block_send.at[distance + lanes, group], block_sem.at[source, group], (seq, lane + distance)
+        )
+
+    def inside(distance):
+        return jnp.logical_and(lane + distance >= 0, lane + distance < lanes)
+
+    def onward(group, action):
+        for distance in range(2, lanes - 1):
+            for sign in (1, -1):
+                @when(inside(-sign * distance), inside(sign))
+                def _():
+                    copy = remote(
+                        att.at[lane - sign * distance, pl.ds(pl.multiple_of(group * width, width), width)],
+                        att.at[lane - sign * distance, pl.ds(pl.multiple_of(group * width, width), width)],
+                        relay_send.at[sign * distance + lanes, group],
+                        block_sem.at[lane - sign * distance, group],
+                        (seq, lane + sign),
+                    )
+                    if action:
+                        copy.wait_recv()
+                        copy.start()
+                    else:
+                        copy.wait_send()
 
     barrier = pltpu.get_barrier_semaphore()
     pl.semaphore_signal(barrier, inc=1, device_id=(sibling, lane), device_id_type=MESH)
@@ -152,7 +134,7 @@
     for step in range(1, lanes):
         pl.semaphore_signal(barrier, inc=1, device_id=(seq, (lane + step) % lanes), device_id_type=MESH)
 
-    own = pltpu.make_async_copy(kv_ref, held.at[seq], load_sem.at[0])
+    own = pltpu.make_async_copy(qkv_ref, wq, load_sem.at[0])
     own.start()
     own_shard = pltpu.make_async_copy(shard_ref, wo.at[lane], load_sem.at[1])
     own_shard.start()
@@ -162,43 +144,68 @@
     ]
     for load in loads:
         load.start()
+    normed = term
+
+    @pl.loop(0, rows // sub)
+    def _(index):
+        span = pl.ds(pl.multiple_of(index * sub, sub), sub)
+        normed[span, :] = layer_norm(tokens_ref[span, :].astype(jnp.float32), first_gain_ref[...]).astype(normed.dtype)
+
+    pl.semaphore_wait(barrier, chips + lanes - 1)
+    own_shard.wait()
+    for step in range(1, lanes):
+        wide(lane, step).start()
     own.wait()
-    pl.semaphore_wait(barrier, chips + lanes - 1)
+
+    def project(which):
+        return lax.dot_general(
+            wq[which], normed[...], (((0,), (1,)), ((), ())), preferred_element_type=jnp.float32
+        )
+
+    for which in (1, 2):
+        result = project(which).astype(jnp.bfloat16)
+        for group in range(groups):
+            strip = result[group * width : (group + 1) * width]
+            held[seq, group, (which - 1) * size : which * size] = strip.reshape(size, HD, rows)
 
     def open_group(group):
         exchange(group, 0, 0).start()
         hand(group, 0, core).start()
 
-    open_group(0)
-    own_shard.wait()
-    for step in range(1, lanes):
-        wide(lane, step).start()
+    for group in range(groups):
+        open_group(group)
+    query[...] = (project(0) * (LOG2E / HD**0.5)).astype(jnp.bfloat16).reshape(query.shape)
+
+    def early(group):
+        hand(group, 1, core).wait_recv()
+        hand(group, 1, core).start()
+        for stage in range(1, bits):
+            exchange(group, 1, stage).start()
+
+        @pl.when(group + 1 < groups)
+        def _():
+            for stage in range(1, bits):
+                exchange(group + 1, 0, stage).start()
 
     def prepare(group, index):
         arrival, second = index // 2, index % 2
         which = core + second - 2 * core * second
-        hand(group, arrival, which).wait_recv()
-
-        @pl.when(second == 0)
+
+        @pl.when(index != 2)
+        def _():
+            hand(group, arrival, which).wait_recv()
+
+        @when(second == 0, arrival > 1)
         def _():
             hand(group, arrival, core).start()
-            for stage in range(1, bits):
+            for stage in range(2, bits):
                 @pl.when(arrival < 2**stage)
                 def _():
                     exchange(group, arrival, stage).start()
 
-        @when(second == 0, arrival == 1)
-        def _():
-            for stage in range(1, bits):
-                exchange(group, 0, stage).start()
-
-            @pl.when(group + 1 < groups)
-            def _():
-                open_group(group + 1)
-
     def score(slot, group, member, target):
         result = lax.dot_general(
-            held[slot, group, member], q_ref[group * size + member], CONTRACT_FIRST,
+            held[slot, group, member], query[group * size + member], CONTRACT_FIRST,
             preferred_element_type=jnp.float32,
         )
         target[...] = result
@@ -206,66 +213,86 @@
 
     def attend(slot, group, member, source, top):
         value = held[slot, group, size + member]
+        head = group * size + member
         value = jnp.concatenate([value, jnp.ones((ONES, rows), value.dtype)], axis=0)
-        old = peak[member]
+        old = peak[head]
         new = jnp.maximum(old, top)
         weights = jnp.exp2(source[...] - new).astype(jnp.bfloat16)
         term_here = jnp.dot(value, weights, preferred_element_type=jnp.float32)
-        accum[member] = accum[member] * jnp.exp2(old - new) + term_here
-        peak[member] = new
+        accum[head] = accum[head] * jnp.exp2(old - new) + term_here
+        peak[head] = new
 
     scores = (score_a, score_b)
     column[...] = score(seq, 0, 0, score_a)
 
-    @pl.loop(0, groups)
-    def _(group):
-        accum[...] = jnp.zeros_like(accum)
-        peak[...] = jnp.full_like(peak, -1e30)
-
-        @pl.loop(0, n)
-        def _(index):
-            def place(position):
-                arrival, second = position // 2, position % 2
-                return slot_of(arrival, core + second - 2 * core * second)
-
-            @pl.when(index == chips)
+    accum[...] = jnp.zeros_like(accum)
+    peak[...] = jnp.full_like(peak, -1e30)
+    local, total_turns = 2 * groups, n * groups
+
+    def locate(turn):
+        later = turn - local
+        group = jnp.where(turn < local, turn // 2, later // (n - 2))
+        index = jnp.where(turn < local, turn % 2, 2 + later % (n - 2))
+        arrival, second = index // 2, index % 2
+        return group, index, slot_of(arrival, core + second - 2 * core * second)
+
+    @pl.loop(0, total_turns)
+    def _(turn):
+        group, index, slot = locate(turn)
+
+        @pl.when(turn == min(2, local - 1))
+        def _():
+            for stage in range(1, bits):
+                exchange(0, 0, stage).start()
+
+        @pl.when(turn == min(4, local - 1))
+        def _():
+            early(0)
+
+        @when(index == 3, group + 1 < groups)
+        def _():
+            early(group + 1)
+
+        @when(index == 4, group == max(groups - 2, 0))
+        def _():
+            for step in range(1, lanes):
+                source = (lane + step) % lanes
+                wide(source, step).wait_recv()
+                share(source, part).start()
+                for other in range(1, mates):
+                    spread(source, other).start()
+
+        for member in range(size):
+            top = column[...]
+            if member < size - 1:
+                below = score(slot, group, member + 1, scores[(member + 1) % 2])
+            else:
+                next_group, next_index, next_slot = locate(jnp.minimum(turn + 1, total_turns - 1))
+
+                @when(turn + 1 < total_turns, next_index > 0)
+                def _():
+                    prepare(next_group, next_index)
+
+                below = score(next_slot, next_group, 0, scores[(member + 1) % 2])
+            attend(slot, group, member, scores[member % 2], top)
+            column[...] = below
+
+        @pl.when(index == n - 1)
+        def _():
+            for member in range(size):
+                head = group * size + member
+                rows_here = pl.ds(pl.multiple_of(head * HD, HD), HD)
+                att[lane, rows_here, :] = (accum[head, :HD] / accum[head, HD : HD + 1]).astype(att.dtype)
+            for distance in (1, -1, 2, -2):
+                @pl.when(inside(distance))
+                def _():
+                    block(lane, group, distance).start()
+
+            @pl.when(group > 0)
             def _():
-                tick_middle(group)
-
-            @when(index == 3, group == groups - 1)
-            def _():
-                for step in range(1, lanes):
-                    source = (lane + step) % lanes
-                    wide(source, step).wait_recv()
-                    share(source, part).start()
-                    for other in range(1, mates):
-                        spread(source, other).start()
-
-            slot = place(index)
-            for member in range(size):
-                top = column[...]
-                if member < size - 1:
-                    below = score(slot, group, member + 1, scores[(member + 1) % 2])
-                else:
-                    @pl.when(index + 1 < n)
-                    def _():
-                        prepare(group, index + 1)
-
-                    last = index + 1 == n
-                    following = jnp.where(last, seq, place((index + 1) % n))
-                    next_group = jnp.minimum(group + jnp.where(last, 1, 0), groups - 1)
-                    below = score(following, next_group, 0, scores[(member + 1) % 2])
-                attend(slot, group, member, scores[member % 2], top)
-                column[...] = below
-
-        for member in range(size):
-            rows_here = pl.ds(pl.multiple_of(group * width + member * HD, HD), HD)
-            att[lane, rows_here, :] = (accum[member, :HD] / accum[member, HD : HD + 1]).astype(att.dtype)
-        tick_end(group)
-
-    for group in range(groups, groups + lanes // 2 + 1):
-        tick_middle(group)
-        tick_end(group)
+                onward(group - 1, True)
+
+    onward(groups - 1, True)
 
     for step in range(1, lanes):
         source = (lane + step) % lanes
@@ -277,11 +304,22 @@
         source = (lane + step) % lanes
         for other in range(mates):
             share(source, (mate(other) * 2 + 1 - core) % parts).wait_recv()
+    for group in range(groups):
+        for distance in (1, 2, *range(3, lanes)):
+            for sign in (1, -1):
+                if distance < 2 or distance == lanes - 1:
+                    arrived = inside(sign * distance)
+                else:
+                    arrived = jnp.logical_and(inside(sign * distance), jnp.logical_not(inside(-sign)))
+
+                @pl.when(arrived)
+                def _():
+                    block(lane + sign * distance, group, 1).wait_recv()
     for load in loads:
         load.wait()
 
     full, rest = rows // chunk, rows % chunk
-    chunks, per, pieces = full + (rest > 0), chunk // sub, rows // sub
+    chunks, pieces = full + (rest > 0), rows // sub
     middle = lanes // 2
     on_left = lane < middle
     depth = jnp.where(on_left, lane, lanes - 1 - lane)
@@ -351,14 +389,9 @@
 
         store(index).start()
 
-    def each(step, body):
-        @pl.when(jnp.logical_and(step >= 0, step < chunks))
-        def _():
-            @pl.loop(step * per, jnp.minimum(step * per + per, pieces))
-            def _(index):
-                body(index)
-
-    @pl.loop(0, chunks + lanes - 1)
+    lag = 2
+
+    @pl.loop(0, chunks + middle - 1)
     def _(step):
         @pl.when(step < full)
         def _():
@@ -369,17 +402,24 @@
             def _():
                 compute(full * chunk, rest)
 
-        each(step - depth, reduce_inward)
-
-        @pl.when(central)
-        def _():
-            each(step - middle, finish)
-
-        @when(jnp.logical_not(central), depth > 0)
-        def _():
-            each(step - middle - (middle - 1 - depth), relay)
-
-    @when(jnp.logical_not(central), depth == 0)
+        behind = step - depth
+
+        @when(behind >= 0, behind < chunks)
+        def _():
+            @pl.loop(behind * chunk // sub, jnp.minimum(behind * chunk + chunk, rows) // sub)
+            def _(index):
+                reduce_inward(index)
+
+                @when(central, index >= lag)
+                def _():
+                    finish(index - lag)
+
+    @pl.when(central)
+    def _():
+        for index in range(pieces - lag, pieces):
+            finish(index)
+
+    @pl.when(jnp.logical_not(central))
     def _():
         @pl.loop(0, pieces)
         def _(index):
@@ -387,14 +427,13 @@
 
     @pl.loop(0, groups)
     def _(group):
-        for source in range(lanes):
-            @when(lane >= source, has_right)
+        for distance in (1, -1, 2, -2):
+            @pl.when(inside(distance))
             def _():
-                block(source, group, lane + 1, right_sem).wait_send()
-
-            @when(lane <= source, has_left)
-            def _():
-                block(source, group, lane - 1, left_sem).wait_send()
+                block(lane, group, distance).wait_send()
+
+        onward(group, False)
+
 
         for arrival in range(chips):
             hand(group, arrival, core).wait_send()
@@ -420,33 +459,37 @@
             outward(index).wait_send()
 
 
-def fused(n, lanes, query, pairs, tokens, gain, w_out, w_up, w_down):
+def fused(n, lanes, tokens, first_gain, w_qkv, gain, w_out, w_up, w_down):
     rows, width = tokens.shape
     span, hidden = w_out.shape[0], w_up.shape[1]
     heads = span // HD
-    groups, size = pairs.shape[0], pairs.shape[1] // 2
+    size = 2
+    groups = heads // size
     parts = n
     while span // parts % 16 or span % parts:
         parts //= 2
     chips = n // 2
     bits = chips.bit_length() - 1
-    chunk, sub = 128, 16
+    chunk = 128
+    sub = max(size for size in (16, 32, 48) if rows % size == 0)
     pieces = rows // sub
     vmem = pl.BlockSpec(memory_space=pltpu.VMEM)
     hbm = pl.BlockSpec(memory_space=pl.ANY)
     dma = pltpu.SemaphoreType.DMA
     return pl.pallas_call(
-        functools.partial(layer_kernel, n, lanes, parts, chunk, sub),
+        functools.partial(layer_kernel, n, lanes, parts, chunk, sub, groups, size),
         out_shape=jax.ShapeDtypeStruct((rows, width), jnp.bfloat16),
-        in_specs=[vmem, vmem, vmem, vmem, hbm, hbm, hbm],
+        in_specs=[vmem, vmem, hbm, vmem, hbm, hbm, hbm],
         out_specs=hbm,
         scratch_shapes=[
+            pltpu.VMEM((heads, HD, rows), jnp.bfloat16),
+            pltpu.VMEM(w_qkv.shape, jnp.bfloat16),
             pltpu.VMEM((n, groups, 2 * size, HD, rows), jnp.bfloat16),
             pltpu.VMEM((rows, rows), jnp.float32),
             pltpu.VMEM((rows, rows), jnp.float32),
             pltpu.VMEM((1, rows), jnp.float32),
-            pltpu.VMEM((size, HD + ONES, rows), jnp.float32),
-            pltpu.VMEM((size, 1, rows), jnp.float32),
+            pltpu.VMEM((heads, HD + ONES, rows), jnp.float32),
+            pltpu.VMEM((heads, 1, rows), jnp.float32),
             pltpu.VMEM((lanes, span, rows), jnp.bfloat16),
             pltpu.VMEM((lanes, span, width), jnp.bfloat16),
             pltpu.VMEM((width, hidden), jnp.bfloat16),
@@ -465,8 +508,8 @@
             dma((lanes, parts)),
             dma((lanes, parts)),
             dma((lanes, groups)),
-            dma((lanes, groups)),
-            dma((lanes, groups)),
+            dma((2 * lanes, groups)),
+            dma((2 * lanes, groups)),
             dma((pieces,)),
             dma((2, pieces)),
             dma((pieces,)),
@@ -481,21 +524,12 @@
             bytes_accessed=2 * width * (lanes * span + 2 * hidden),
             transcendentals=n * heads * rows * rows,
         ),
-    )(query, pairs, tokens, gain, w_out, w_up, w_down)
+    )(tokens, first_gain, w_qkv, gain, w_out, w_up, w_down)
 
 
 def per_device(n, lanes, tokens, norm_gain, w_qkv, w_out, post_gain, w_up, w_down):
-    rows = tokens.shape[0]
-    span = w_qkv.shape[2]
-    heads = span // HD
-    base = tokens.astype(jnp.float32)
-    normed = layer_norm(base, norm_gain).astype(jnp.bfloat16)
-    weights = w_qkv.reshape(w_qkv.shape[0], -1)
-    qkv = lax.dot_general(weights, normed, (((0,), (1,)), ((), ())), preferred_element_type=jnp.float32)
-    query = (qkv[:span] * (LOG2E / HD**0.5)).astype(jnp.bfloat16).reshape(heads, HD, rows)
-    pairs = qkv[span:].astype(jnp.bfloat16).reshape(2, heads // 2, 2, HD, rows)
-    pairs = pairs.transpose(1, 0, 2, 3, 4).reshape(heads // 2, 4, HD, rows)
-    return fused(n, lanes, query, pairs, tokens, post_gain.reshape(1, -1), w_out, w_up, w_down)
+    w_qkv = w_qkv.transpose(1, 0, 2)
+    return fused(n, lanes, tokens, norm_gain, w_qkv, post_gain, w_out, w_up, w_down)
 
 
 def solution(mesh):

time: 218 us -> 147 us (0.67)
  Pallas kernels: 191 us -> 144 us
  local copies, waits for them, and re-layouts: 14.5 us -> 3.12 us
  matrix products: 6.89 us -> 0 us
  other arithmetic: 4.2 us -> 0 us
    pallas_call x1, Pallas kernels: 191 us -> 144 us  [fused(): pl.pallas_call(functools.partial(layer_kernel, n, lanes, parts, chunk, su...]
    dot_general x1 -> x0, matrix products: 6.89 us -> none  [per_device(): lax.dot_general(weights, normed, (((0,), (1,)), ((), ())), preferred_elem...]
    unnamed x8 -> x1, local copies, waits for them, and re-layouts: 9.36 us -> 3.12 us
    reduce_sum x2 -> x0, other arithmetic: 2.84 us -> none  [the longest x1 2.13 us: layer_norm(): mean = jnp.mean(values, axis=-1, keepdims=True)]
    slice x2 -> x0, local copies, waits for them, and re-layouts: 2.37 us -> none  [per_device(): pairs = qkv[span:].astype(jnp.bfloat16).reshape(2, heads // 2, 2, HD, rows)]
where the time goes in v1:
time: 147 us
  Pallas kernels  144 us (98%)
  local copies, waits for them, and re-layouts  3.12 us (2%)
    pallas_call x1, Pallas kernels, fused(): pl.pallas_call(functools.partial(layer_kernel, n, lanes, parts, chunk, su...  144 us
    unnamed x1, local copies, waits for them, and re-layouts  3.12 us

profile of v1, /device:TPU:0, one launch (start us, length us, event | category | flops | bytes accessed | tf_op | source)
XLA Modules:
  0.0 147.1 jit_solution(10218184797719254820)
XLA Ops:
  0.0 143.9 %shard_map.73 = bf16[720,1536]{1,0:T(8,128)(2,1)} custom-call(bf16[720,1536]{1,0:T(8,128)(2,1)} %tokens_ref.1, f32[1536]{0:T(1024)} %first_gain_ref.1, bf16[3,1536,384]{2,1,0:T(8,128)(2,1)} %bitcast.1, f32[1536]{0:T(1024)} %gain_ref.1, bf16[384,1536]{1,0:T(8,128)(2,1)} %shard_ref.1, bf16[1536,1536]{1,0:T(8,128)(2,1)} %up_ref.1, bf16[1536,1536]{1,0:T(8,128)(2,1)} %down_ref.1), custom_call_target="tpu_custom_call" | custom-call | flops 16562257920 | bytes 14155776 | tf_op jit(solution)/shard_map/pallas_call | solution.py:479
  143.9 3.1 %copy.9 = bf16[720,1536]{1,0:T(8,128)(2,1)} copy(bf16[720,1536]{1,0:T(8,128)(2,1)} %shard_map.73) | data formatting | bytes 4423680

commit v2 on v1

--- a/solution.py
+++ b/solution.py
@@ -173,7 +173,9 @@
         hand(group, 0, core).start()
 
     for group in range(groups):
-        open_group(group)
+        hand(group, 0, core).start()
+    for group in range(min(2, groups)):
+        exchange(group, 0, 0).start()
     query[...] = (project(0) * (LOG2E / HD**0.5)).astype(jnp.bfloat16).reshape(query.shape)
 
     def early(group):
@@ -181,6 +183,10 @@
         hand(group, 1, core).start()
         for stage in range(1, bits):
             exchange(group, 1, stage).start()
+
+        @pl.when(group + 2 < groups)
+        def _():
+            exchange(group + 2, 0, 0).start()
 
         @pl.when(group + 1 < groups)
         def _():
@@ -262,20 +268,22 @@
                 for other in range(1, mates):
                     spread(source, other).start()
 
+        next_group, next_index, next_slot = locate(jnp.minimum(turn + 1, total_turns - 1))
+
+        @when(turn + 1 < total_turns, next_index > 0)
+        def _():
+            prepare(next_group, next_index)
+
+        top = column[...]
         for member in range(size):
-            top = column[...]
             if member < size - 1:
                 below = score(slot, group, member + 1, scores[(member + 1) % 2])
             else:
-                next_group, next_index, next_slot = locate(jnp.minimum(turn + 1, total_turns - 1))
-
-                @when(turn + 1 < total_turns, next_index > 0)
-                def _():
-                    prepare(next_group, next_index)
-
                 below = score(next_slot, next_group, 0, scores[(member + 1) % 2])
             attend(slot, group, member, scores[member % 2], top)
-            column[...] = below
+            top = below
+
+        column[...] = top
 
         @pl.when(index == n - 1)
         def _():
@@ -283,7 +291,7 @@
                 head = group * size + member
                 rows_here = pl.ds(pl.multiple_of(head * HD, HD), HD)
                 att[lane, rows_here, :] = (accum[head, :HD] / accum[head, HD : HD + 1]).astype(att.dtype)
-            for distance in (1, -1, 2, -2):
+            for distance in (2, -2, 1, -1):
                 @pl.when(inside(distance))
                 def _():
                     block(lane, group, distance).start()

time: 147 us -> 145 us (0.986)
  Pallas kernels: 144 us -> 141 us
    pallas_call x1, Pallas kernels: 144 us -> 141 us  [fused(): pl.pallas_call(functools.partial(layer_kernel, n, lanes, parts, chunk, su...]
where the time goes in v2:
time: 145 us; the launch traced here: 144 us
  Pallas kernels  141 us (97%)
  local copies, waits for them, and re-layouts  3.12 us (2%)
    pallas_call x1, Pallas kernels, fused(): pl.pallas_call(functools.partial(layer_kernel, n, lanes, parts, chunk, su...  141 us
    unnamed x1, local copies, waits for them, and re-layouts  3.12 us

profile of v2, /device:TPU:0, one launch (start us, length us, event | category | flops | bytes accessed | tf_op | source)
XLA Modules:
  0.0 144.5 jit_solution(14926895505263661065)
XLA Ops:
  0.0 141.3 %shard_map.73 = bf16[720,1536]{1,0:T(8,128)(2,1)} custom-call(bf16[720,1536]{1,0:T(8,128)(2,1)} %tokens_ref.1, f32[1536]{0:T(1024)} %first_gain_ref.1, bf16[3,1536,384]{2,1,0:T(8,128)(2,1)} %bitcast.1, f32[1536]{0:T(1024)} %gain_ref.1, bf16[384,1536]{1,0:T(8,128)(2,1)} %shard_ref.1, bf16[1536,1536]{1,0:T(8,128)(2,1)} %up_ref.1, bf16[1536,1536]{1,0:T(8,128)(2,1)} %down_ref.1), custom_call_target="tpu_custom_call" | custom-call | flops 16562257920 | bytes 14155776 | tf_op jit(solution)/shard_map/pallas_call | solution.py:487
  141.4 3.1 %copy.9 = bf16[720,1536]{1,0:T(8,128)(2,1)} copy(bf16[720,1536]{1,0:T(8,128)(2,1)} %shard_map.73) | data formatting | bytes 4423680
